TPU v7x, 128 devices: a whole 4x4x4 slice. The times are simulated.
128 devices in a mesh: dp: 8 (over z, core), tp: 16 (over y, x).
Axes of the slice: x: 4, y: 4, z: 4, core: 2. Of those that a mesh axis runs over, the one named last changes fastest.
Arguments:
- head_fsdp: bfloat16 [4096, 128256], P(('dp', 'tp')), may hold values from -0.5 to 0.5
- hidden: bfloat16 [2048, 4096], P(('dp', 'tp')), may hold values from -48 to 48
- targets: int32 [2048], P(('dp', 'tp')), may hold values from 0 to 128255
Outputs:
- head_tp: bfloat16 [4096, 128256], P('dp', 'tp')
- log_norm: float32 [2048], P(('dp', 'tp'))
- target_logprob: float32 [2048], P(('dp', 'tp'))
All inputs are finite; a program needn't handle non-finite values.
Results may differ from a plain program's by a relative error of at most 0.0004.
Values may be sent and summed in bfloat16 or wider, within the bound.
No kernel may reach another device: no remote copies, remote signals or barrier semaphores. Data moves between devices by JAX's collectives and lax.ppermute only.
A program may use at most 192 MiB of HBM per device.

v0:
```python
import jax
import jax.numpy as jnp
from jax import lax
from jax.sharding import Mesh
from jax.sharding import PartitionSpec as P

TP = ("tp_0", "tp_1")
DP = ("dp_0", "dp_1")
DP_TP = ("dp_0", "dp_1", "tp_0", "tp_1")


def all_in_one(shard, axis):
    leaves = jax.tree.leaves(shard)
    order = sorted(range(len(leaves)), key=lambda k: -leaves[k].size)
    width = (1, *leaves[order[0]].shape)[-1]
    lines = [
        jnp.pad(leaves[k].reshape(-1), (0, -leaves[k].size % width)).reshape(-1, width)
        for k in order
    ]
    both, at, found = (lax.all_gather(jnp.concatenate(lines), axis), 0, {})
    for k, line in zip(order, lines):
        piece = both[:, at : at + len(line)].reshape(len(both), -1)
        found[k] = piece[:, : leaves[k].size].reshape(-1, *leaves[k].shape)
        at += len(line)
    numbers = iter(range(len(leaves)))
    return jax.tree.map(lambda _: found[next(numbers)], shard)


def joined_all(shard, axes, combine):
    for axis in axes:
        pieces = all_in_one(shard, axis)
        shard = jax.tree.map(lambda part: part[0], pieces)
        for k in range(1, lax.axis_size(axis)):
            shard = combine(shard, jax.tree.map(lambda part: part[k], pieces))
    return shard


def combine_rows(earlier, later):
    peak_one, mass_one, pick_one = earlier
    peak_two, mass_two, pick_two = later
    highest = jnp.maximum(peak_one, peak_two)
    joined = mass_one * jnp.exp(peak_one - highest) + mass_two * jnp.exp(peak_two - highest)
    return (highest, joined, pick_one + pick_two)


def shards(head_fsdp, hidden, targets):
    head_tp = lax.all_to_all(head_fsdp, TP, split_axis=1, concat_axis=0, tiled=True)
    head_full = lax.all_to_all(head_tp, DP, split_axis=1, concat_axis=0, tiled=True)
    vocab_start = lax.axis_index(TP) * head_tp.shape[1] + lax.axis_index(DP) * head_full.shape[1]
    all_hidden, all_targets = (
        lax.all_gather(hidden, DP_TP, axis=0, tiled=True),
        lax.all_gather(targets, DP_TP, axis=0, tiled=True),
    )
    logits = jnp.dot(all_hidden, head_full, preferred_element_type=jnp.float32)
    local_peak = jnp.max(logits, axis=1)
    offset = all_targets - vocab_start
    columns = lax.broadcasted_iota(jnp.int32, logits.shape, 1)
    picked = jnp.sum(jnp.where(columns == offset[:, None], logits, 0.0), axis=1)
    local_mass = jnp.sum(jnp.exp(logits - local_peak[:, None]), axis=1)
    top_logit, total_mass, target_logit = joined_all(
        (local_peak, local_mass, picked), DP_TP, combine_rows
    )
    log_norm = top_logit + jnp.log(total_mass)
    logprob = target_logit - log_norm
    own_rows = hidden.shape[0]
    row_start = (lax.axis_index(DP) * lax.axis_size(TP) + lax.axis_index(TP)) * own_rows
    own_norm = lax.dynamic_slice_in_dim(log_norm, row_start, own_rows, 0)
    own_logprob = lax.dynamic_slice_in_dim(logprob, row_start, own_rows, 0)
    return (head_tp, own_norm, own_logprob)


def solution(mesh):
    split = Mesh(mesh.devices.reshape(4, 2, 4, 4), ("dp_0", "dp_1", "tp_0", "tp_1"))
    placed = (P(DP_TP, None), P(DP_TP, None), P(DP_TP))
    return jax.shard_map(
        shards,
        mesh=split,
        in_specs=placed,
        out_specs=(P(DP, TP), P(DP_TP), P(DP_TP)),
        check_vma=False,
    )
```

profile of v0, /device:TPU:0, one launch (start us, length us, event | category | flops | bytes accessed | tf_op | source)
XLA Modules:
  0.0 437.6 jit_solution(9103793541087411088)
XLA Ops:
  7.2 0.0 all-gather.10.cloned.1.call-start
  7.2 0.7 all-gather.10.cloned.1.call-update
  7.9 14.4 %all_to_all.28 = bf16[32,16,8016]{2,1,0:T(8,128)(2,1)} reshape(bf16[32,128256]{1,0:T(8,128)(2,1)} %param.3) | data formatting | bytes 16416768 | tf_op jit(solution)/shard_map/all_to_all | solution.py:47
  22.3 8.0 %copy.10 = bf16[32,16,8016]{2,0,1:T(8,128)(2,1)} copy(bf16[32,16,8016]{2,1,0:T(8,128)(2,1)} %all_to_all.28) | data formatting | bytes 16416768 | tf_op jit(solution)/shard_map/all_to_all | solution.py:47
  30.3 129.8 %all_to_all.38 = bf16[32,16,8016]{2,0,1:T(8,128)(2,1)} all-to-all(bf16[32,16,8016]{2,0,1:T(8,128)(2,1)} %copy.10), channel_id=1, replica_groups=mesh['dp_0'=4,'dp_1'=2,'tp_0'=4,'tp_1'=4] {'tp_0','tp_1'}, dimensions={1} | all-to-all | bytes 16416768 | tf_op jit(solution)/shard_map/all_to_all | solution.py:47
  160.1 18.6 %all_to_all.32 = bf16[512,8,1002]{2,1,0:T(8,128)(2,1)} reshape(bf16[16,32,8016]{2,1,0:T(8,128)(2,1)} %bitcast.203) | data formatting | bytes 16416768 | tf_op jit(solution)/shard_map/all_to_all | solution.py:48
  178.7 12.5 %copy.11 = bf16[512,8,1002]{0,2,1:T(8,128)(2,1)} copy(bf16[512,8,1002]{2,1,0:T(8,128)(2,1)} %all_to_all.32) | data formatting | bytes 16416768 | tf_op jit(solution)/shard_map/all_to_all | solution.py:48
  191.2 0.0 copy-start
  191.2 5.4 %all-to-all-start.1 = ((bf16[512,8,1002]{0,2,1:T(8,128)(2,1)}), bf16[512,8,1002]{0,2,1:T(8,128)(2,1)}, u32[]{:S(2)}, u32[]{:S(2)}) async-start(bf16[512,8,1002]{0,2,1:T(8,128)(2,1)} %copy.11), calls=%async_computation.1 | async-start | bytes 16515072 | tf_op jit(solution)/shard_map/all_to_all | solution.py:48
  196.6 0.0 copy-done
  196.6 0.3 dynamic-update-slice
  196.9 146.1 %all-reduce = s32[2048]{0:T(1024)S(1)} all-reduce(s32[2048]{0:T(1024)S(1)} %dynamic-update-slice), channel_id=1, replica_groups=mesh['dp_0'=4,'dp_1'=2,'tp_0'=4,'tp_1'=4] {'dp_0','dp_1','tp_0','tp_1'}, use_global_device_ids=true, to_apply=%add | all-reduce | flops 2048 | bytes 16384
  342.9 11.7 %copy.13 = bf16[512,8016]{0,1:T(8,128)(2,1)} copy(bf16[512,8016]{1,0:T(8,128)(2,1)} %bitcast.204) | data formatting | bytes 16416768
  354.6 0.0 all-to-all-done.1
  354.6 12.1 %copy.12 = bf16[8,512,1002]{2,1,0:T(8,128)(2,1)} copy(bf16[8,512,1002]{1,2,0:T(8,128)(2,1)} %bitcast.2) | data formatting | bytes 16416768 | tf_op jit(solution)/shard_map/all_to_all | solution.py:48
  366.8 0.0 all-gather.10.cloned.1.call-done
  366.8 22.6 %fusion.41 = (f32[2048]{0:T(1024)S(1)}, f32[2048,1002]{0,1:T(8,128)S(1)}) fusion(bf16[2048,4096]{1,0:T(8,128)(2,1)} %all-gather.10.cloned.1.call-done, bf16[4096,1002]{1,0:T(8,128)(2,1)} %bitcast.205), kind=kOutput, calls=%fused_computation.81 | convolution fusion | flops 16812820480 | bytes 33202176 | tf_op jit(solution)/shard_map/dot_general | solution.py:54
  389.4 2.3 exponential_reduce_fusion
  391.7 12.0 %all-gather.4 = f32[4,3,2048]{2,1,0:T(4,128)S(1)} all-gather(f32[1,3,2048]{2,1,0:T(4,128)S(1)} %maximum_bitcast_fusion), channel_id=2, replica_groups=mesh['dp_0'=4,'dp_1'=2,'tp_0'=4,'tp_1'=4] {'dp_0'}, dimensions={0}, use_global_device_ids=true | all-gather | bytes 122880 | tf_op jit(solution)/shard_map/all_gather | solution.py:20
  403.8 0.1 fusion.16
  403.9 1.9 all-gather.5
  405.8 12.0 %all-gather.6 = f32[4,3,2048]{2,1,0:T(4,128)S(1)} all-gather(f32[1,3,2048]{2,1,0:T(4,128)S(1)} %maximum_bitcast_fusion.2), channel_id=4, replica_groups=mesh['dp_0'=4,'dp_1'=2,'tp_0'=4,'tp_1'=4] {'tp_0'}, dimensions={0}, use_global_device_ids=true | all-gather | bytes 122880 | tf_op jit(solution)/shard_map/all_gather | solution.py:20
  417.9 0.1 fusion.2
  418.0 12.0 %all-gather.7 = f32[4,3,2048]{2,1,0:T(4,128)S(1)} all-gather(f32[1,3,2048]{2,1,0:T(4,128)S(1)} %maximum_bitcast_fusion.3), channel_id=5, replica_groups=mesh['dp_0'=4,'dp_1'=2,'tp_0'=4,'tp_1'=4] {'tp_1'}, dimensions={0}, use_global_device_ids=true | all-gather | bytes 122880 | tf_op jit(solution)/shard_map/all_gather | solution.py:20
  430.0 0.1 fusion.40
  430.1 0.6 dynamic-slice_subtract_fusion
  (11 shorter events, 0.3 us)
Async XLA Ops:
  7.2 359.6 %all-gather.10.cloned.1.call-start = ((), (), s32[]{:S(2)}) async-start(), calls=%async_computation.2 | async-start | bytes 16908288 | tf_op jit(solution)/shard_map/all_gather | solution.py:51
  191.2 5.4 %copy-start = (s32[16]{0:T(128)S(1)}, s32[16]{0:T(128)}, u32[]{:S(2)}) copy-start(s32[16]{0:T(128)} %param.5) | copy-start | bytes 196
  191.2 163.5 %all-to-all-start.1 = ((bf16[512,8,1002]{0,2,1:T(8,128)(2,1)}), bf16[512,8,1002]{0,2,1:T(8,128)(2,1)}, u32[]{:S(2)}, u32[]{:S(2)}) async-start(bf16[512,8,1002]{0,2,1:T(8,128)(2,1)} %copy.11), calls=%async_computation.1 | async-start | bytes 16515072 | tf_op jit(solution)/shard_map/all_to_all | solution.py:48
Sparse Core Ops, SparseCore 0:
  11.1 148.0 all-gather.9
where the time goes:
time: 439 us; the launch traced here: 438 us
  blocking collectives  314 us (72%)
  local copies, waits for them, and re-layouts  77.6 us (18%)
  matrix products  22.6 us (5%)
  between operations  14.1 us (3%)
  starting transfers between devices  5.43 us (1%)
    unnamed x1, blocking collectives  146 us
    all_to_all x1, blocking collectives, shards(): lax.all_to_all(head_fsdp, TP, split_axis=1, concat_axis=0, tiled=True)  130 us
    all_to_all x3, local copies, waits for them, and re-layouts, shards(): lax.all_to_all(head_tp, DP, split_axis=1, concat_axis=0, tiled=True)  43.2 us
    all_gather x4, blocking collectives, all_in_one(): both, at, found = (lax.all_gather(jnp.concatenate(lines), axis), 0, {})  37.8 us
    dot_general x1, matrix products, shards(): logits = jnp.dot(all_hidden, head_full, preferred_element_type=jnp.float32)  22.6 us
    all_to_all x2, local copies, waits for them, and re-layouts, shards(): lax.all_to_all(head_fsdp, TP, split_axis=1, concat_axis=0, tiled=True)  22.4 us
    unnamed x5, local copies, waits for them, and re-layouts  12 us
  transfers between devices with their start and end apart: 2, of which 0 were waited for; matrix products, arithmetic and copies ran while one was open for 10% of the time, Pallas kernels for 0%

commit v1 on v0

v1 whole, which is shorter than its diff:
```python
import jax
import jax.numpy as jnp
from jax import lax
from jax.experimental import pallas as pl
from jax.experimental.pallas import tpu as pltpu
from jax.sharding import Mesh
from jax.sharding import PartitionSpec as P

AXES = ("z", "c", "y", "x")
ROWS = 32
BLOCK = 8016
TP = 16
WIDTHS = (3072, 3072, 2048)
STARTS = (0, 3072, 6144)
GROUPS = (1, 1, 1)
D = 4096
LANES = 128
NEG = -3.0e38


def any_spec():
    return pl.BlockSpec(memory_space=pl.ANY)


def cut_body(off, width, head, out, buf, made, sem, gone):
    total = head.shape[1]
    plan = []
    for t in range(TP):
        start = t * BLOCK + off
        base = start // LANES * LANES
        end = min(-(-(start + width) // LANES) * LANES, total)
        plan.append((start - base, base, end - base))
    copies = [
        pltpu.make_async_copy(head.at[:, pl.ds(base, span)], buf.at[t, :, pl.ds(0, span)], sem.at[t])
        for t, (_, base, span) in enumerate(plan)
    ]
    sends = [pltpu.make_async_copy(made.at[t], out.at[t], gone.at[t]) for t in range(TP)]
    for c in copies:
        c.start()
    for t, (shift, _, span) in enumerate(plan):
        copies[t].wait()
        have = min(width, span - shift)
        whole = buf[t, :, :span]
        if shift:
            whole = pltpu.roll(whole, span - shift, 1)
        if have == width:
            made[t] = whole[:, :width]
        else:
            low = have // LANES * LANES
            made[t, :, :low] = whole[:, :low]
            tail = whole[:, low : low + LANES]
            lane = lax.broadcasted_iota(jnp.int32, tail.shape, 1)
            made[t, :, low : low + LANES] = jnp.where(lane < have - low, tail, jnp.zeros_like(tail))
            if low + LANES < width:
                made[t, :, low + LANES :] = jnp.zeros((ROWS, width - low - LANES), out.dtype)
        sends[t].start()
    for s in sends:
        s.wait()


def cut(head, off, width):
    return pl.pallas_call(
        lambda *refs: cut_body(off, width, *refs),
        out_shape=jax.ShapeDtypeStruct((TP, ROWS, width), head.dtype),
        in_specs=[pl.BlockSpec(memory_space=pltpu.HBM)],
        out_specs=pl.BlockSpec(memory_space=pltpu.HBM),
        scratch_shapes=[
            pltpu.VMEM((TP, ROWS, width + LANES), head.dtype),
            pltpu.VMEM((TP, ROWS, width), head.dtype),
            pltpu.SemaphoreType.DMA((TP,)),
            pltpu.SemaphoreType.DMA((TP,)),
        ],
    )(head)


def join_body(targets, hidden, out):
    out[:, :D] = hidden[...]
    row = lax.broadcasted_iota(jnp.int32, (16, LANES), 0)
    lane = lax.broadcasted_iota(jnp.int32, (16, LANES), 1)
    digits = jnp.zeros((16, LANES), jnp.int32)
    for r in range(16):
        value = targets[r]
        for place, digit in enumerate((value & 255, (value >> 8) & 255, value >> 16)):
            digits = jnp.where((row == r) & (lane == place), digit, digits)
    out[:, D:] = digits.astype(jnp.float32).astype(out.dtype)


def join(hidden, targets):
    return pl.pallas_call(
        join_body,
        out_shape=jax.ShapeDtypeStruct((16, D + LANES), hidden.dtype),
        in_specs=[pl.BlockSpec(memory_space=pltpu.SMEM), pl.BlockSpec(memory_space=pltpu.VMEM)],
        out_specs=pl.BlockSpec(memory_space=pltpu.VMEM),
        name="join",
    )(targets, hidden)


def turn(got, old, z, off):
    rows, width = got.shape
    part = width // 4
    valid = min(width, BLOCK - off)
    last = valid - 3 * part
    order = (1, 3, 2, 0)

    def body(info, got, *refs):
        refs = refs if old is None else refs[1:]
        head, *pieces = refs[:5]
        buf, made, sem, gone, kept = refs[5:]
        places = [lax.rem(info[0] + j, 4) for j in range(4)]
        copies = [
            pltpu.make_async_copy(
                got.at[:, pl.ds(pl.multiple_of(places[j] * part, LANES), part)], buf.at[j], sem.at[j]
            )
            for j in range(4)
        ]
        for j in order:
            copies[j].start()
        sends, keeps = [], []
        for j in order:
            copies[j].wait()
            made[j] = buf[j].T
            send = pltpu.make_async_copy(made.at[j], pieces[j], gone.at[j])
            send.start()
            sends.append(send)
            to = off + pl.multiple_of(places[j] * part, LANES)
            if last == part:
                keep = pltpu.make_async_copy(made.at[j], head.at[pl.ds(to, part), :], kept.at[j])
                keep.start()
                keeps.append(keep)
            else:
                full = pltpu.make_async_copy(made.at[j], head.at[pl.ds(to, part), :], kept.at[j])
                some = pltpu.make_async_copy(
                    made.at[j, pl.ds(0, last), :], head.at[pl.ds(off + 3 * part, last), :], kept.at[j]
                )
                pl.when(places[j] != 3)(full.start)
                pl.when(places[j] == 3)(some.start)
                keeps.append((places[j], full, some))
        for send in sends:
            send.wait()
        for keep in keeps:
            if last == part:
                keep.wait()
            else:
                pl.when(keep[0] != 3)(keep[1].wait)
                pl.when(keep[0] == 3)(keep[2].wait)

    return pl.pallas_call(
        body,
        in_specs=[pl.BlockSpec(memory_space=pltpu.SMEM), any_spec()] + ([] if old is None else [any_spec()]),
        out_specs=[any_spec()] * 5,
        out_shape=[jax.ShapeDtypeStruct((BLOCK, rows), got.dtype)]
        + [jax.ShapeDtypeStruct((part, rows), got.dtype)] * 4,
        scratch_shapes=[
            pltpu.VMEM((4, rows, part), got.dtype),
            pltpu.VMEM((4, part, rows), got.dtype),
            pltpu.SemaphoreType.DMA((4,)),
            pltpu.SemaphoreType.DMA((4,)),
            pltpu.SemaphoreType.DMA((4,)),
        ],
        input_output_aliases={} if old is None else {2: 0},
    )(z, got, *([] if old is None else [old]))


STEPS = 8
SLAB = D // STEPS
HALF = 512
QUARTER = 128


def score_body(plan, first, info, hid, *refs):
    count = len(plan)
    weights, refs = refs[: count * STEPS], refs[count * STEPS :]
    old = None
    if not first:
        old, refs = refs[0], refs[1:]
    new, logit, sem = refs[:3]
    tables = refs[3:]
    m = hid.shape[0]
    loads = [
        [
            pltpu.make_async_copy(
                weights[g * STEPS + j],
                tables[g].at[:, pl.ds(pl.multiple_of(info[j] * SLAB, SLAB), SLAB)],
                sem.at[g * STEPS + j],
            )
            for j in range(STEPS)
        ]
        for g in range(count)
    ]

    for load in loads[0]:
        load.start()
    for group in loads[1:]:
        for load in group:
            load.start()
    for g, (width, masked) in enumerate(plan):
        start, limit = info[STEPS + 2 * g], info[STEPS + 2 * g + 1]
        for load in loads[g]:
            load.wait()

        def half(i, done):
            logit[:, :width] = lax.dot_general(
                hid[pl.ds(pl.multiple_of(i * HALF, HALF), HALF), :D],
                tables[g][...],
                (((1,), (1,)), ((), ())),
                preferred_element_type=jnp.float32,
            )

            def stats(b, carry):
                at = pl.multiple_of(b * QUARTER, QUARTER)
                to = pl.multiple_of(i * HALF + b * QUARTER, QUARTER)
                logits = logit[pl.ds(at, QUARTER), :width]
                digits = hid[pl.ds(to, QUARTER), D:].astype(jnp.int32)
                target = digits[:, 0:1] + digits[:, 1:2] * 256 + digits[:, 2:3] * 65536 - start
                target = jnp.where(target < limit, target, -1)
                column = lax.broadcasted_iota(jnp.int32, logits.shape, 1)
                pick = jnp.sum(jnp.where(column == target, logits, 0.0), axis=1, keepdims=True)
                if masked:
                    logits = jnp.where(column < limit, logits, NEG)
                peak = jnp.max(logits, axis=1, keepdims=True)
                merge = not first or g > 0
                if merge:
                    before = (old if g == 0 else new)[pl.ds(to, QUARTER), :]
                    peak = jnp.maximum(peak, before[:, 0:1])
                mass = jnp.sum(jnp.exp(logits - peak), axis=1, keepdims=True)
                if merge:
                    mass = mass + before[:, 1:2] * jnp.exp(before[:, 0:1] - peak)
                    pick = pick + before[:, 2:3]
                lane = lax.broadcasted_iota(jnp.int32, (QUARTER, LANES), 1)
                new[pl.ds(to, QUARTER), :] = jnp.where(lane == 0, peak, jnp.where(lane == 1, mass, pick))
                return carry

            return lax.fori_loop(0, HALF // QUARTER, stats, done)

        lax.fori_loop(0, m // HALF, half, 0)


def score(hidden, weights, old, info, plan):
    m = hidden.shape[0]
    widths = [width for width, _ in plan]
    first = old is None
    vmem = pl.BlockSpec(memory_space=pltpu.VMEM)
    return pl.pallas_call(
        lambda *refs: score_body(plan, first, *refs),
        in_specs=[pl.BlockSpec(memory_space=pltpu.SMEM), vmem, *[any_spec()] * len(weights)]
        + ([] if first else [vmem]),
        out_specs=vmem,
        scratch_shapes=[
            pltpu.VMEM((HALF, max(widths)), jnp.float32),
            pltpu.SemaphoreType.DMA((len(weights),)),
            *[pltpu.VMEM((width, D), hidden.dtype) for width in widths],
        ],
        out_shape=jax.ShapeDtypeStruct((m, LANES), jnp.float32),
        cost_estimate=pl.CostEstimate(
            flops=2 * m * D * sum(widths), bytes_accessed=2 * (m + sum(widths)) * D, transcendentals=m * sum(widths)
        ),
        compiler_params=pltpu.CompilerParams(vmem_limit_bytes=24 << 20),
    )(info, hidden, *weights, *([] if first else [old]))


def around(n, k):
    return [(i, (i + k) % n) for i in range(n)]


def shards(head, hidden, targets):
    z, c = lax.axis_index("z"), lax.axis_index("c")
    block = lax.axis_index(("y", "x"))
    slabs = [lax.rem(z + 4 - j, 4) * 2 + lax.rem(c + e, 2) for e in range(2) for j in range(4)]
    mine = join(hidden, targets)
    every = lax.all_gather(mine, ("z", "y", "x"), axis=0, tiled=True)
    stats, flat, waiting, group = None, None, [], 0
    for width, off in zip(WIDTHS, STARTS):
        sent = cut(head, off, width)
        got = lax.all_to_all(sent, ("y", "x"), split_axis=0, concat_axis=0, tiled=True)
        got = got.reshape(TP * ROWS, width)
        flat, *pieces = turn(got, flat, z.reshape(1), off)
        for j in range(1, 4):
            pieces[j] = lax.ppermute(pieces[j], "z", around(4, j))
        other = []
        for j in range(4):
            other.append(lax.ppermute(pieces[j], "c", around(2, 1)))
        part = width // 4
        valid = min(width, BLOCK - off)
        waiting.append((pieces + other, block * BLOCK + off + z * part, valid - z * part, (part, valid < width)))
        if len(waiting) == GROUPS[group]:
            info = jnp.stack([*slabs, *[v for w in waiting for v in w[1:3]]]).astype(jnp.int32)
            stats = score(every, [p for w in waiting for p in w[0]], stats, info, [w[3] for w in waiting])
            waiting, group = [], group + 1
    table = stats[:, :3].reshape(64, 16, 3).transpose(0, 2, 1).reshape(64, 48)
    table = lax.all_to_all(table, ("z", "y", "x"), split_axis=0, concat_axis=0, tiled=True)
    table = table.reshape(64, 3, 16)
    peak = jnp.max(table[:, 0], axis=0)
    mass = jnp.sum(table[:, 1] * jnp.exp(table[:, 0] - peak), axis=0)
    norm = peak + jnp.log(mass)
    return flat.T, norm, jnp.sum(table[:, 2], axis=0) - norm


def solution(mesh):
    devices = Mesh(mesh.devices.reshape(4, 2, 4, 4), AXES)
    return jax.shard_map(
        shards,
        mesh=devices,
        in_specs=(P(AXES, None), P(AXES, None), P(AXES)),
        out_specs=(P(("z", "c"), ("y", "x")), P(AXES), P(AXES)),
        check_vma=False,
    )
```

time: 439 us -> 340 us (0.77)
  blocking collectives: 314 us -> 19.6 us
  waiting for transfers between devices: 0.69 us -> 199 us
  local copies, waits for them, and re-layouts: 77.6 us -> 16.3 us
  Pallas kernels: 0 us -> 60.3 us
  starting transfers between devices: 5.43 us -> 28.6 us
  matrix products: 22.6 us -> 0 us
    unnamed x1 -> x0, blocking collectives: 146 us -> none
    all_to_all x1 -> x3, waiting for transfers between devices: 0.01 us -> 120 us  [shards(): lax.all_to_all(sent, ('y', 'x'), split_axis=0, concat_axis=0, tiled=True)]
    all_to_all x1, blocking collectives: 130 us -> 19.6 us  [shards(): lax.all_to_all(table, ('z', 'y', 'x'), split_axis=0, concat_axis=0, tiled...]
    ppermute x0 -> x21, waiting for transfers between devices: none -> 79.7 us  [the longest x9 79.6 us: shards(): pieces[j] = lax.ppermute(pieces[j], 'z', around(4, j))]
    all_to_all x5 -> x2, local copies, waits for them, and re-layouts: 65.6 us -> 0.15 us  [shards(): lax.all_to_all(table, ('z', 'y', 'x'), split_axis=0, concat_axis=0, tiled...]
    pallas_call x0 -> x10, Pallas kernels: none -> 60.3 us  [the longest x3 36.1 us: score(): pl.pallas_call(lambda *refs: score_body(plan, first, *refs), in_specs=[pl...]
    all_gather x4 -> x0, blocking collectives: 37.8 us -> none  [all_in_one(): both, at, found = (lax.all_gather(jnp.concatenate(lines), axis), 0, {})]
    dot_general x1 -> x0, matrix products: 22.6 us -> none  [shards(): logits = jnp.dot(all_hidden, head_full, preferred_element_type=jnp.float32)]
  transfers between devices with their start and end apart: 2 -> 25, of which waited for: 0 -> 7; matrix products, arithmetic and copies ran while one was open for 10% -> 0% of each run, Pallas kernels for 0% -> 14%
where the time goes in v1:
time: 340 us; the launch traced here: 339 us
  waiting for transfers between devices  199 us (59%)
  Pallas kernels  60.3 us (18%)
  starting transfers between devices  28.6 us (8%)
  blocking collectives  19.6 us (6%)
  local copies, waits for them, and re-layouts  16.3 us (5%)
  between operations  14.4 us (4%)
    all_to_all x3, waiting for transfers between devices, shards(): lax.all_to_all(sent, ('y', 'x'), split_axis=0, concat_axis=0, tiled=True)  120 us
    ppermute x9, waiting for transfers between devices, shards(): pieces[j] = lax.ppermute(pieces[j], 'z', around(4, j))  79.6 us
    pallas_call x3, Pallas kernels, score(): pl.pallas_call(lambda *refs: score_body(plan, first, *refs), in_specs=[pl...  36.1 us
    all_to_all x1, blocking collectives, shards(): lax.all_to_all(table, ('z', 'y', 'x'), split_axis=0, concat_axis=0, tiled...  19.6 us
    all_to_all x3, starting transfers between devices, shards(): lax.all_to_all(sent, ('y', 'x'), split_axis=0, concat_axis=0, tiled=True)  18.7 us
    unnamed x42, local copies, waits for them, and re-layouts  15.7 us
    pallas_call x3, Pallas kernels, turn(): pl.pallas_call(body, in_specs=[pl.BlockSpec(memory_space=pltpu.SMEM), any...  11.8 us
    pallas_call x3, Pallas kernels, cut(): pl.pallas_call(lambda *refs: cut_body(off, width, *refs), out_shape=jax.S...  10.9 us
  transfers between devices with their start and end apart: 25, of which 7 were waited for; matrix products, arithmetic and copies ran while one was open for 0% of the time, Pallas kernels for 14%

profile of v1, /device:TPU:0, one launch (start us, length us, event | category | flops | bytes accessed | tf_op | source)
XLA Modules:
  0.0 339.5 jit_solution(6565203906905728113)
XLA Ops:
  7.2 1.6 join.1
  8.9 3.7 %shard_map.60 = bf16[16,32,3072]{2,1,0:T(8,128)(2,1)} custom-call(bf16[32,128256]{1,0:T(8,128)(2,1)} %refs_0_.5), custom_call_target="tpu_custom_call" | custom-call | tf_op jit(solution)/shard_map/pallas_call | solution.py:62
  12.6 7.2 %all-to-all-start.2 = ((bf16[16,32,3072]{2,1,0:T(8,128)(2,1)}), bf16[16,32,3072]{2,1,0:T(8,128)(2,1)S(1)}, u32[]{:S(2)}, u32[]{:S(2)}) async-start(bf16[16,32,3072]{2,1,0:T(8,128)(2,1)} %shard_map.60), calls=%async_computation.2 | async-start | bytes 6291456 | tf_op jit(solution)/shard_map/all_to_all | solution.py:274
  19.8 3.7 %shard_map.59 = bf16[16,32,3072]{2,1,0:T(8,128)(2,1)} custom-call(bf16[32,128256]{1,0:T(8,128)(2,1)} %refs_0_.5), custom_call_target="tpu_custom_call" | custom-call | tf_op jit(solution)/shard_map/pallas_call | solution.py:62
  23.5 45.0 %all-to-all-done.2 = bf16[16,32,3072]{2,1,0:T(8,128)(2,1)S(1)} async-done(((bf16[16,32,3072]{2,1,0:T(8,128)(2,1)}), bf16[16,32,3072]{2,1,0:T(8,128)(2,1)S(1)}, u32[]{:S(2)}, u32[]{:S(2)}) %all-to-all-start.2) | async-done | bytes 3145760 | tf_op jit(solution)/shard_map/all_to_all | solution.py:274
  68.5 4.5 %all-to-all-start.1 = ((bf16[16,32,3072]{2,1,0:T(8,128)(2,1)}), bf16[16,32,3072]{2,1,0:T(8,128)(2,1)}, u32[]{:S(2)}, u32[]{:S(2)}) async-start(bf16[16,32,3072]{2,1,0:T(8,128)(2,1)} %shard_map.59), calls=%async_computation.1 | async-start | bytes 6291456 | tf_op jit(solution)/shard_map/all_to_all | solution.py:274
  73.0 3.4 %shard_map.58 = bf16[16,32,2048]{2,1,0:T(8,128)(2,1)} custom-call(bf16[32,128256]{1,0:T(8,128)(2,1)} %refs_0_.5), custom_call_target="tpu_custom_call" | custom-call | tf_op jit(solution)/shard_map/pallas_call | solution.py:62
  76.4 54.8 %all-to-all-done.1 = bf16[16,32,3072]{2,1,0:T(8,128)(2,1)} async-done(((bf16[16,32,3072]{2,1,0:T(8,128)(2,1)}), bf16[16,32,3072]{2,1,0:T(8,128)(2,1)}, u32[]{:S(2)}, u32[]{:S(2)}) %all-to-all-start.1) | async-done | bytes 3145760 | tf_op jit(solution)/shard_map/all_to_all | solution.py:274
  131.3 7.1 %all-to-all-start = ((bf16[16,32,2048]{2,1,0:T(8,128)(2,1)}), bf16[16,32,2048]{2,1,0:T(8,128)(2,1)S(1)}, u32[]{:S(2)}, u32[]{:S(2)}) async-start(bf16[16,32,2048]{2,1,0:T(8,128)(2,1)} %shard_map.58), calls=%async_computation | async-start | bytes 4194304 | tf_op jit(solution)/shard_map/all_to_all | solution.py:274
  138.4 4.2 %shard_map.61 = (bf16[8016,512]{1,0:T(8,128)(2,1)}, bf16[768,512]{1,0:T(8,128)(2,1)}, bf16[768,512]{1,0:T(8,128)(2,1)}, bf16[768,512]{1,0:T(8,128)(2,1)}, bf16[768,512]{1,0:T(8,128)(2,1)}) custom-call(s32[1]{0:T(128)} %bitcast.info, bf16[512,3072]{1,0:T(8,128)(2,1)} %bitcast.40), custom_call_target="tpu_custom_call" | custom-call | tf_op jit(solution)/shard_map/pallas_call | solution.py:147
  142.6 4.2 %shard_map.62 = (bf16[8016,512]{1,0:T(8,128)(2,1)}, bf16[768,512]{1,0:T(8,128)(2,1)}, bf16[768,512]{1,0:T(8,128)(2,1)}, bf16[768,512]{1,0:T(8,128)(2,1)}, bf16[768,512]{1,0:T(8,128)(2,1)}) custom-call(s32[1]{0:T(128)} %bitcast.info, bf16[512,3072]{1,0:T(8,128)(2,1)} %bitcast.2.got, ...), custom_call_target="tpu_custom_call", output_to_operand_aliasing={{0}: (2, {})} | custom-call | tf_op jit(solution)/shard_map/pallas_call | solution.py:147
  146.7 19.8 %all-to-all-done = bf16[16,32,2048]{2,1,0:T(8,128)(2,1)S(1)} async-done(((bf16[16,32,2048]{2,1,0:T(8,128)(2,1)}), bf16[16,32,2048]{2,1,0:T(8,128)(2,1)S(1)}, u32[]{:S(2)}, u32[]{:S(2)}) %all-to-all-start) | async-done | bytes 2097184 | tf_op jit(solution)/shard_map/all_to_all | solution.py:274
  166.6 1.3 copy-done.17
  167.9 3.4 %shard_map.63 = (bf16[8016,512]{1,0:T(8,128)(2,1)}, bf16[512,512]{1,0:T(8,128)(2,1)}, bf16[512,512]{1,0:T(8,128)(2,1)}, bf16[512,512]{1,0:T(8,128)(2,1)}, bf16[512,512]{1,0:T(8,128)(2,1)}) custom-call(s32[1]{0:T(128)} %bitcast.info, bf16[512,2048]{1,0:T(8,128)(2,1)} %bitcast.41, ...), custom_call_target="tpu_custom_call", output_to_operand_aliasing={{0}: (2, {})} | custom-call | tf_op jit(solution)/shard_map/pallas_call | solution.py:147
  171.4 2.7 collective-permute-start.1
  174.1 1.3 collective-permute-start.14
  175.5 0.9 collective-permute-start.15
  176.4 1.8 collective-permute-start.16
  178.1 20.7 %collective-permute-done.refs_3_ = bf16[512,512]{1,0:T(8,128)(2,1)S(1)} collective-permute-done((bf16[512,512]{1,0:T(8,128)(2,1)}, bf16[512,512]{1,0:T(8,128)(2,1)S(1)}, u32[]{:S(2)}, u32[]{:S(2)}) %collective-permute-start) | collective-permute-done | bytes 524320 | tf_op jit(solution)/shard_map/ppermute | solution.py:278
  198.8 0.8 copy-done.14
  199.6 32.9 %collective-permute-done.14.refs_3_ = bf16[768,512]{1,0:T(8,128)(2,1)S(1)} collective-permute-done((bf16[768,512]{1,0:T(8,128)(2,1)}, bf16[768,512]{1,0:T(8,128)(2,1)S(1)}, u32[]{:S(2)}, u32[]{:S(2)}) %collective-permute-start.14) | collective-permute-done | bytes 786464 | tf_op jit(solution)/shard_map/ppermute | solution.py:278
  232.7 0.9 copy-done.3
  233.5 0.9 copy-done.7
  234.4 0.5 collective-permute-start.19
  234.9 0.9 copy-done.5
  235.8 10.6 %collective-permute-done.7.refs_3_ = bf16[768,512]{1,0:T(8,128)(2,1)S(1)} collective-permute-done((bf16[768,512]{1,0:T(8,128)(2,1)}, bf16[768,512]{1,0:T(8,128)(2,1)S(1)}, u32[]{:S(2)}, u32[]{:S(2)}) %collective-permute-start.7) | collective-permute-done | bytes 786464 | tf_op jit(solution)/shard_map/ppermute | solution.py:278
  246.5 15.4 %collective-permute-done.8.refs_4_ = bf16[768,512]{1,0:T(8,128)(2,1)} collective-permute-done((bf16[768,512]{1,0:T(8,128)(2,1)}, bf16[768,512]{1,0:T(8,128)(2,1)}, u32[]{:S(2)}, u32[]{:S(2)}) %collective-permute-start.8) | collective-permute-done | bytes 786464 | tf_op jit(solution)/shard_map/ppermute | solution.py:278
  261.9 0.5 collective-permute-start.11
  262.4 0.9 copy-done.9
  263.4 0.9 copy-done.11
  264.2 0.4 collective-permute-start.13
  264.9 0.3 collective-permute-start.2
  265.2 3.4 %copy-done = bf16[1024,4224]{1,0:T(8,128)(2,1)S(1)} copy-done((bf16[1024,4224]{1,0:T(8,128)(2,1)S(1)}, bf16[1024,4224]{1,0:T(8,128)(2,1)}, u32[]{:S(2)}) %copy-start) | copy-done | bytes 8650776
  268.7 1.1 copy-done.4
  269.8 1.1 copy-done.6
  270.9 1.1 copy-done.8
  272.1 1.1 copy-done.10
  273.2 1.1 copy-done.12
  274.4 11.8 %shard_map.64.refs_10_ = f32[1024,128]{1,0:T(8,128)S(1)} custom-call(s32[10]{0:T(128)S(1)} %stack.80.refs_0_, bf16[1024,4224]{1,0:T(8,128)(2,1)S(1)} %copy-done, bf16[768,512]{1,0:T(8,128)(2,1)S(1)} %copy-done.2, bf16[768,512]{1,0:T(8,128)(2,1)S(1)} %copy-done.4, bf16[768,512]{1,0:T(8,128)(2,1)S(1)} %copy-done.6, ...), custom_call_target="tpu_custom_call" | custom-call | flops 6442450944 | bytes 14680064 | tf_op jit(solution)/shard_map/pallas_call | solution.py:243
  286.2 0.2 collective-permute-start.3
  286.4 0.4 collective-permute-start.4
  286.9 0.4 collective-permute-start.6
  287.3 14.2 %shard_map.65.refs_10_ = f32[1024,128]{1,0:T(8,128)S(1)} custom-call(s32[10]{0:T(128)S(1)} %stack.78.refs_0_, bf16[1024,4224]{1,0:T(8,128)(2,1)S(1)} %copy-done, bf16[768,512]{1,0:T(8,128)(2,1)S(1)} %copy-done.1, bf16[768,512]{1,0:T(8,128)(2,1)S(1)} %collective-permute-done.7.refs_3_, bf16[768,512]{1,0:T(8,128)(2,1)} %collective-permute-done.8.refs_4_, ...), custom_call_target="tpu_custom_call" | custom-call | flops 6442450944 | bytes 14680064 | tf_op jit(solution)/shard_map/pallas_call | solution.py:243
  301.6 10.1 %shard_map.66 = f32[1024,128]{1,0:T(8,128)S(1)} custom-call(s32[10]{0:T(128)S(1)} %stack.75.refs_0_, bf16[1024,4224]{1,0:T(8,128)(2,1)S(1)} %bitcast.38, bf16[512,512]{1,0:T(8,128)(2,1)S(1)} %copy-done.13, bf16[512,512]{1,0:T(8,128)(2,1)S(1)} %collective-permute-done.refs_3_, bf16[512,512]{1,0:T(8,128)(2,1)S(1)} %copy-done.15, ...), custom_call_target="tpu_custom_call" | custom-call | flops 4294967296 | bytes 12582912 | tf_op jit(solution)/shard_map/pallas_call | solution.py:243
  311.7 0.3 copy.10
  312.1 19.6 %all_to_all.24 = f32[64,1,48]{2,1,0:T(1,128)S(1)} all-to-all(f32[64,1,48]{2,1,0:T(1,128)S(1)} %copy.11), channel_id=1, replica_groups=mesh['z'=4,'c'=2,'y'=4,'x'=4] {'z','y','x'}, dimensions={0} | all-to-all | bytes 24576 | tf_op jit(solution)/shard_map/all_to_all | solution.py:290
  331.9 0.2 fusion.1
  332.1 0.5 fusion.3
  (66 shorter events, 1.1 us)
Async XLA Ops:
  7.2 258.0 %all-gather.2.cloned.1.call-start = ((), (), s32[]{:S(2)}) async-start(), calls=%async_computation.4 | async-start | bytes 8785920 | tf_op jit(solution)/shard_map/all_gather | solution.py:270
  12.6 55.9 %all-to-all-start.2 = ((bf16[16,32,3072]{2,1,0:T(8,128)(2,1)}), bf16[16,32,3072]{2,1,0:T(8,128)(2,1)S(1)}, u32[]{:S(2)}, u32[]{:S(2)}) async-start(bf16[16,32,3072]{2,1,0:T(8,128)(2,1)} %shard_map.60), calls=%async_computation.2 | async-start | bytes 6291456 | tf_op jit(solution)/shard_map/all_to_all | solution.py:274
  68.5 7.9 %copy-start.16 = (bf16[16,32,3072]{2,1,0:T(8,128)(2,1)}, bf16[16,32,3072]{2,1,0:T(8,128)(2,1)S(1)}, u32[]{:S(2)}) copy-start(bf16[16,32,3072]{2,1,0:T(8,128)(2,1)S(1)} %all-to-all-done.2) | copy-start | bytes 9437188
  68.5 62.8 %all-to-all-start.1 = ((bf16[16,32,3072]{2,1,0:T(8,128)(2,1)}), bf16[16,32,3072]{2,1,0:T(8,128)(2,1)}, u32[]{:S(2)}, u32[]{:S(2)}) async-start(bf16[16,32,3072]{2,1,0:T(8,128)(2,1)} %shard_map.59), calls=%async_computation.1 | async-start | bytes 6291456 | tf_op jit(solution)/shard_map/all_to_all | solution.py:274
  131.3 35.3 %all-to-all-start = ((bf16[16,32,2048]{2,1,0:T(8,128)(2,1)}), bf16[16,32,2048]{2,1,0:T(8,128)(2,1)S(1)}, u32[]{:S(2)}, u32[]{:S(2)}) async-start(bf16[16,32,2048]{2,1,0:T(8,128)(2,1)} %shard_map.58), calls=%async_computation | async-start | bytes 4194304 | tf_op jit(solution)/shard_map/all_to_all | solution.py:274
  166.6 1.3 copy-start.17
  167.9 31.0 %copy-start.2 = (bf16[768,512]{1,0:T(8,128)(2,1)S(1)}, bf16[768,512]{1,0:T(8,128)(2,1)}, u32[]{:S(2)}) copy-start(bf16[768,512]{1,0:T(8,128)(2,1)} %get-tuple-element.29.refs_2_) | copy-start | bytes 2359300
  167.9 94.0 %copy-start.1 = (bf16[768,512]{1,0:T(8,128)(2,1)S(1)}, bf16[768,512]{1,0:T(8,128)(2,1)}, u32[]{:S(2)}) copy-start(bf16[768,512]{1,0:T(8,128)(2,1)} %get-tuple-element.25.refs_2_) | copy-start | bytes 2359300
  171.3 27.5 %collective-permute-start = (bf16[512,512]{1,0:T(8,128)(2,1)}, bf16[512,512]{1,0:T(8,128)(2,1)S(1)}, u32[]{:S(2)}, u32[]{:S(2)}) collective-permute-start(bf16[512,512]{1,0:T(8,128)(2,1)} %get-tuple-element.22), channel_id=1, source_target_pairs={{0,32},{32,64},{64,96},{96,0},{1,33},{33,65},{65,97},{97,1},{2,34}... | collective-permute-start | bytes 1572872 | tf_op jit(solution)/shard_map/ppermute | solution.py:278
  171.4 27.5 %collective-permute-start.1 = (bf16[512,512]{1,0:T(8,128)(2,1)}, bf16[512,512]{1,0:T(8,128)(2,1)S(1)}, u32[]{:S(2)}, u32[]{:S(2)}) collective-permute-start(bf16[512,512]{1,0:T(8,128)(2,1)} %get-tuple-element.23), channel_id=1, source_target_pairs={{0,64},{32,96},{64,0},{96,32},{1,65},{33,97},{65,1},{97,33},{2,66}... | collective-permute-start | bytes 1572872 | tf_op jit(solution)/shard_map/ppermute | solution.py:278
  174.1 58.4 %collective-permute-start.14 = (bf16[768,512]{1,0:T(8,128)(2,1)}, bf16[768,512]{1,0:T(8,128)(2,1)S(1)}, u32[]{:S(2)}, u32[]{:S(2)}) collective-permute-start(bf16[768,512]{1,0:T(8,128)(2,1)} %get-tuple-element.30), channel_id=1, source_target_pairs={{0,32},{32,64},{64,96},{96,0},{1,33},{33,65},{65,97},{97,1},{2,34}... | collective-permute-start | bytes 2359304 | tf_op jit(solution)/shard_map/ppermute | solution.py:278
  175.5 57.1 %collective-permute-start.15 = (bf16[768,512]{1,0:T(8,128)(2,1)}, bf16[768,512]{1,0:T(8,128)(2,1)S(1)}, u32[]{:S(2)}, u32[]{:S(2)}) collective-permute-start(bf16[768,512]{1,0:T(8,128)(2,1)} %get-tuple-element.31), channel_id=1, source_target_pairs={{0,64},{32,96},{64,0},{96,32},{1,65},{33,97},{65,1},{97,33},{2,66}... | collective-permute-start | bytes 2359304 | tf_op jit(solution)/shard_map/ppermute | solution.py:278
  176.4 56.2 %collective-permute-start.16 = (bf16[768,512]{1,0:T(8,128)(2,1)}, bf16[768,512]{1,0:T(8,128)(2,1)}, u32[]{:S(2)}, u32[]{:S(2)}) collective-permute-start(bf16[768,512]{1,0:T(8,128)(2,1)} %get-tuple-element.32), channel_id=1, source_target_pairs={{0,96},{32,0},{64,32},{96,64},{1,97},{33,1},{65,33},{97,65},{2,98}... | collective-permute-start | bytes 2359304 | tf_op jit(solution)/shard_map/ppermute | solution.py:278
  198.8 34.7 %collective-permute-start.17 = (bf16[768,512]{1,0:T(8,128)(2,1)S(1)}, bf16[768,512]{1,0:T(8,128)(2,1)S(1)}, u32[]{:S(2)}, u32[]{:S(2)}) collective-permute-start(bf16[768,512]{1,0:T(8,128)(2,1)S(1)} %copy-done.2), channel_id=1, source_target_pairs={{0,16},{16,0},{1,17},{17,1},{2,18},{18,2},{3,19},{19,3},{4,20},{20... | collective-permute-start | bytes 2359304 | tf_op jit(solution)/shard_map/ppermute | solution.py:281
  198.8 0.8 copy-start.14
  199.6 46.8 %collective-permute-start.7 = (bf16[768,512]{1,0:T(8,128)(2,1)}, bf16[768,512]{1,0:T(8,128)(2,1)S(1)}, u32[]{:S(2)}, u32[]{:S(2)}) collective-permute-start(bf16[768,512]{1,0:T(8,128)(2,1)} %get-tuple-element.26), channel_id=1, source_target_pairs={{0,32},{32,64},{64,96},{96,0},{1,33},{33,65},{65,97},{97,1},{2,34}... | collective-permute-start | bytes 2359304 | tf_op jit(solution)/shard_map/ppermute | solution.py:278
  232.5 29.3 %collective-permute-start.8 = (bf16[768,512]{1,0:T(8,128)(2,1)}, bf16[768,512]{1,0:T(8,128)(2,1)}, u32[]{:S(2)}, u32[]{:S(2)}) collective-permute-start(bf16[768,512]{1,0:T(8,128)(2,1)} %get-tuple-element.27), channel_id=1, source_target_pairs={{0,64},{32,96},{64,0},{96,32},{1,65},{33,97},{65,1},{97,33},{2,66}... | collective-permute-start | bytes 2359304 | tf_op jit(solution)/shard_map/ppermute | solution.py:278
  232.5 29.3 %collective-permute-start.9 = (bf16[768,512]{1,0:T(8,128)(2,1)}, bf16[768,512]{1,0:T(8,128)(2,1)}, u32[]{:S(2)}, u32[]{:S(2)}) collective-permute-start(bf16[768,512]{1,0:T(8,128)(2,1)} %get-tuple-element.28), channel_id=1, source_target_pairs={{0,96},{32,0},{64,32},{96,64},{1,97},{33,1},{65,33},{97,65},{2,98}... | collective-permute-start | bytes 2359304 | tf_op jit(solution)/shard_map/ppermute | solution.py:278
  232.6 29.8 %collective-permute-start.18 = (bf16[768,512]{1,0:T(8,128)(2,1)S(1)}, bf16[768,512]{1,0:T(8,128)(2,1)S(1)}, u32[]{:S(2)}, u32[]{:S(2)}) collective-permute-start(bf16[768,512]{1,0:T(8,128)(2,1)S(1)} %collective-permute-done.14.refs_3_), channel_id=1, source_target_pairs={{0,16},{16,0},{1,17},{17,1},{2,18},{18,2},{3,19},{19,3},{4,20},{20... | collective-permute-start | bytes 2359304 | tf_op jit(solution)/shard_map/ppermute | solution.py:281
  232.7 0.9 copy-start.3
  233.5 0.9 copy-start.7
  234.4 28.9 %collective-permute-start.19 = (bf16[768,512]{1,0:T(8,128)(2,1)S(1)}, bf16[768,512]{1,0:T(8,128)(2,1)S(1)}, u32[]{:S(2)}, u32[]{:S(2)}) collective-permute-start(bf16[768,512]{1,0:T(8,128)(2,1)S(1)} %collective-permute-done.15.refs_4_), channel_id=1, source_target_pairs={{0,16},{16,0},{1,17},{17,1},{2,18},{18,2},{3,19},{19,3},{4,20},{20... | collective-permute-start | bytes 2359304 | tf_op jit(solution)/shard_map/ppermute | solution.py:281
  234.9 0.9 copy-start.5
  246.5 18.5 %collective-permute-start.20 = (bf16[768,512]{1,0:T(8,128)(2,1)}, bf16[768,512]{1,0:T(8,128)(2,1)}, u32[]{:S(2)}, u32[]{:S(2)}) collective-permute-start(bf16[768,512]{1,0:T(8,128)(2,1)} %collective-permute-done.16.refs_5_), channel_id=1, source_target_pairs={{0,16},{16,0},{1,17},{17,1},{2,18},{18,2},{3,19},{19,3},{4,20},{20... | collective-permute-start | bytes 2359304 | tf_op jit(solution)/shard_map/ppermute | solution.py:281
  261.9 24.5 %collective-permute-start.10 = (bf16[768,512]{1,0:T(8,128)(2,1)S(1)}, bf16[768,512]{1,0:T(8,128)(2,1)}, u32[]{:S(2)}, u32[]{:S(2)}) collective-permute-start(bf16[768,512]{1,0:T(8,128)(2,1)S(1)} %copy-done.1), channel_id=1, source_target_pairs={{0,16},{16,0},{1,17},{17,1},{2,18},{18,2},{3,19},{19,3},{4,20},{20... | collective-permute-start | bytes 2359304 | tf_op jit(solution)/shard_map/ppermute | solution.py:281
  261.9 24.9 %collective-permute-start.11 = (bf16[768,512]{1,0:T(8,128)(2,1)S(1)}, bf16[768,512]{1,0:T(8,128)(2,1)}, u32[]{:S(2)}, u32[]{:S(2)}) collective-permute-start(bf16[768,512]{1,0:T(8,128)(2,1)S(1)} %collective-permute-done.7.refs_3_), channel_id=1, source_target_pairs={{0,16},{16,0},{1,17},{17,1},{2,18},{18,2},{3,19},{19,3},{4,20},{20... | collective-permute-start | bytes 2359304 | tf_op jit(solution)/shard_map/ppermute | solution.py:281
  262.4 0.9 copy-start.9
  263.3 23.6 %collective-permute-start.12 = (bf16[768,512]{1,0:T(8,128)(2,1)}, bf16[768,512]{1,0:T(8,128)(2,1)}, u32[]{:S(2)}, u32[]{:S(2)}) collective-permute-start(bf16[768,512]{1,0:T(8,128)(2,1)} %collective-permute-done.8.refs_4_), channel_id=1, source_target_pairs={{0,16},{16,0},{1,17},{17,1},{2,18},{18,2},{3,19},{19,3},{4,20},{20... | collective-permute-start | bytes 2359304 | tf_op jit(solution)/shard_map/ppermute | solution.py:281
  263.4 0.9 copy-start.11
  264.2 23.1 %collective-permute-start.13 = (bf16[768,512]{1,0:T(8,128)(2,1)}, bf16[768,512]{1,0:T(8,128)(2,1)}, u32[]{:S(2)}, u32[]{:S(2)}) collective-permute-start(bf16[768,512]{1,0:T(8,128)(2,1)} %collective-permute-done.9.refs_5_), channel_id=1, source_target_pairs={{0,16},{16,0},{1,17},{17,1},{2,18},{18,2},{3,19},{19,3},{4,20},{20... | collective-permute-start | bytes 2359304 | tf_op jit(solution)/shard_map/ppermute | solution.py:281
  264.9 21.2 %collective-permute-start.2 = (bf16[512,512]{1,0:T(8,128)(2,1)}, bf16[512,512]{1,0:T(8,128)(2,1)}, u32[]{:S(2)}, u32[]{:S(2)}) collective-permute-start(bf16[512,512]{1,0:T(8,128)(2,1)} %get-tuple-element.24), channel_id=1, source_target_pairs={{0,96},{32,0},{64,32},{96,64},{1,97},{33,1},{65,33},{97,65},{2,98}... | collective-permute-start | bytes 1572872 | tf_op jit(solution)/shard_map/ppermute | solution.py:278
  265.2 3.5 %copy-start = (bf16[1024,4224]{1,0:T(8,128)(2,1)S(1)}, bf16[1024,4224]{1,0:T(8,128)(2,1)}, u32[]{:S(2)}) copy-start(bf16[1024,4224]{1,0:T(8,128)(2,1)} %all-gather.2.cloned.1.call-done.refs_1_) | copy-start | bytes 25952260
  268.7 1.1 copy-start.4
  269.8 1.1 copy-start.6
  270.9 1.1 copy-start.8
  272.1 1.1 copy-start.10
  273.2 1.1 copy-start.12
  274.3 11.8 %copy-start.13 = (bf16[512,512]{1,0:T(8,128)(2,1)S(1)}, bf16[512,512]{1,0:T(8,128)(2,1)}, u32[]{:S(2)}) copy-start(bf16[512,512]{1,0:T(8,128)(2,1)} %get-tuple-element.21.refs_2_) | copy-start | bytes 1572868
  274.3 12.5 %copy-start.15 = (bf16[512,512]{1,0:T(8,128)(2,1)S(1)}, bf16[512,512]{1,0:T(8,128)(2,1)}, u32[]{:S(2)}) copy-start(bf16[512,512]{1,0:T(8,128)(2,1)} %copy-done.14) | copy-start | bytes 1572868
  286.2 15.4 %slice-start = ((s8[8650752]{0:T(1024)(128)(4,1)}), s8[4194304]{0:T(1024)(128)(4,1)S(1)}, s32[]{:S(2)}) async-start(s8[8650752]{0:T(1024)(128)(4,1)} %bitcast.37), calls=%async_computation.5 | async-start | bytes 8388608
  286.2 15.4 %slice-start.1 = ((s8[8650752]{0:T(1024)(128)(4,1)}), s8[4194304]{0:T(1024)(128)(4,1)S(1)}, s32[]{:S(2)}) async-start(s8[8650752]{0:T(1024)(128)(4,1)} %bitcast.37), calls=%async_computation.6 | async-start | bytes 8388608
  286.2 15.4 %slice-start.2 = ((s8[8650752]{0:T(1024)(128)(4,1)}), s8[262144]{0:T(1024)(128)(4,1)S(1)}, s32[]{:S(2)}) async-start(s8[8650752]{0:T(1024)(128)(4,1)} %bitcast.37), calls=%async_computation.7 | async-start | bytes 524288
  286.2 15.3 %collective-permute-start.3 = (bf16[512,512]{1,0:T(8,128)(2,1)S(1)}, bf16[512,512]{1,0:T(8,128)(2,1)S(1)}, u32[]{:S(2)}, u32[]{:S(2)}) collective-permute-start(bf16[512,512]{1,0:T(8,128)(2,1)S(1)} %copy-done.13), channel_id=1, source_target_pairs={{0,16},{16,0},{1,17},{17,1},{2,18},{18,2},{3,19},{19,3},{4,20},{20... | collective-permute-start | bytes 1572872 | tf_op jit(solution)/shard_map/ppermute | solution.py:281
  286.4 15.2 %collective-permute-start.4 = (bf16[512,512]{1,0:T(8,128)(2,1)S(1)}, bf16[512,512]{1,0:T(8,128)(2,1)S(1)}, u32[]{:S(2)}, u32[]{:S(2)}) collective-permute-start(bf16[512,512]{1,0:T(8,128)(2,1)S(1)} %collective-permute-done.refs_3_), channel_id=1, source_target_pairs={{0,16},{16,0},{1,17},{17,1},{2,18},{18,2},{3,19},{19,3},{4,20},{20... | collective-permute-start | bytes 1572872 | tf_op jit(solution)/shard_map/ppermute | solution.py:281
  286.8 14.8 %collective-permute-start.5 = (bf16[512,512]{1,0:T(8,128)(2,1)S(1)}, bf16[512,512]{1,0:T(8,128)(2,1)S(1)}, u32[]{:S(2)}, u32[]{:S(2)}) collective-permute-start(bf16[512,512]{1,0:T(8,128)(2,1)S(1)} %copy-done.15), channel_id=1, source_target_pairs={{0,16},{16,0},{1,17},{17,1},{2,18},{18,2},{3,19},{19,3},{4,20},{20... | collective-permute-start | bytes 1572872 | tf_op jit(solution)/shard_map/ppermute | solution.py:281
  286.9 14.7 %collective-permute-start.6 = (bf16[512,512]{1,0:T(8,128)(2,1)}, bf16[512,512]{1,0:T(8,128)(2,1)S(1)}, u32[]{:S(2)}, u32[]{:S(2)}) collective-permute-start(bf16[512,512]{1,0:T(8,128)(2,1)} %collective-permute-done.2.refs_5_), channel_id=1, source_target_pairs={{0,16},{16,0},{1,17},{17,1},{2,18},{18,2},{3,19},{19,3},{4,20},{20... | collective-permute-start | bytes 1572872 | tf_op jit(solution)/shard_map/ppermute | solution.py:281
Sparse Core Ops, SparseCore 0:
  10.7 131.7 all-gather.1
